TPU v7x, 256 devices: a 8x8x2 block of a 8x8x16 slice. The times are simulated.
256 devices in a mesh: sub: 2 (over z), row: 128 (over y, x, core).
Axes of the slice: x: 8, y: 8, z: 2, core: 2. Of those that a mesh axis runs over, the one named last changes fastest.
The devices are a block of a 8x8x16 slice.
Arguments:
- diag_blocks: float32 [4096, 128, 128], P(('sub', 'row')), parts along dimension 0, may hold values from -0.05 to 16, as said below
- coupling: float32 [4096, 3, 128, 128], P(('sub', 'row')), parts along dimension 0, may hold values from -0.05 to 0.05
- offsets: int32 [4096, 3], P(('sub', 'row')), parts along dimension 0, may hold values from 1 to 4, as said below
- mass: float32 [524288], P(('sub', 'row')), parts along dimension 0, may hold values from 0.5 to 2
- initial_modes: float32 [32, 524288], P(None, ('sub', 'row')), parts along dimension 1, may hold values from -6 to 6
Outputs:
- mass_density: float32 [524288], P(('sub', 'row')), parts along dimension 0
- energy_density: float32 [524288], P(('sub', 'row')), parts along dimension 0
There are 2 independent parts, one for each index of `sub`. A program takes and returns all parts, laid end to end along the dimension named above; each array names one. Nothing has to cross between parts.
Inputs may be any that keep to these rules, and one draw needn't show every extreme that they name: `diag_blocks`: each block is symmetric; entries off a block's diagonal lie in -0.05 to 0.05, its diagonal entries in 1 to 16. The 3 offsets of a block row are distinct.
All inputs are finite; a program needn't handle non-finite values.
Results may differ from a plain program's by a relative error of at most 0.0003.
Values sent between devices are 32-bit elements; how exact they have to be, the bound alone decides.
A program may use at most 128 MiB of HBM per device.

v0:
```python
import jax
import jax.numpy as jnp
from jax import lax
from jax.sharding import Mesh
from jax.sharding import PartitionSpec as P

MODES = 32
REACH = 4
ITERS = 3
PURIFY = 28
ROW = ("row_0", "row_1", "row_2")
SUB_ROW = ("sub", "row_0", "row_1", "row_2")
PRECISE = lax.Precision.HIGHEST


def from_behind(value, axis, steps):
    count = lax.axis_size(axis)
    initial, last = (max(0, -steps), min(count, count - steps))
    return lax.ppermute(value, axis, [(source, source + steps) for source in range(initial, last)])


def one_axis_at_a_time(value, axes):
    for axis in axes:
        value = lax.psum(value, axis)
    return value


def one_hot_table(positions, extent):
    return (positions[..., None] == jnp.arange(extent, dtype=jnp.int32)).astype(jnp.float32)


def stiffness_apply(vectors, diag_blocks, coupling, offsets):
    rowcount = vectors.shape[0]
    block_count = diag_blocks.shape[0]
    block_width = diag_blocks.shape[1]
    blocked = vectors.reshape(rowcount, block_count, block_width)
    result = jnp.einsum("nbk,bkj->nbj", blocked, diag_blocks, precision=PRECISE)
    positions = jnp.arange(block_count, dtype=jnp.int32)[:, None] - offsets + REACH
    products = jnp.einsum("nbk,bskj->nbsj", blocked, coupling, precision=PRECISE)
    lower_part = from_behind(vectors[:, (block_count - REACH) * block_width :], ROW, 1)
    extent = block_count + REACH
    extended = jnp.concatenate([lower_part, vectors], axis=1).reshape(rowcount, extent, block_width)
    selector = one_hot_table(positions, extent)
    gathered = jnp.einsum("bse,nek->nbsk", selector, extended, precision=PRECISE)
    result = result + jnp.einsum("nbsk,bsjk->nbj", gathered, coupling, precision=PRECISE)
    spread = jnp.einsum("bse,nbsj->nej", selector, products, precision=PRECISE)
    returned = from_behind(spread[:, :REACH].reshape(rowcount, REACH * block_width), ROW, -1)
    result = result + spread[:, REACH:]
    result = result.at[:, block_count - REACH :].add(returned.reshape(rowcount, REACH, block_width))
    return result.reshape(rowcount, block_count * block_width)


def purify(matrix, occupied, steps_count):
    order = matrix.shape[0]
    identity = jnp.eye(order, dtype=matrix.dtype)
    diagonal = jnp.diagonal(matrix)
    center = jnp.sum(diagonal) / order
    radius = jnp.sum(jnp.abs(matrix), axis=1) - jnp.abs(diagonal)
    highest = jnp.max(diagonal + radius)
    lowest = jnp.min(diagonal - radius)
    factor = jnp.minimum(
        occupied / jnp.maximum(highest - center, 1e-06),
        (order - occupied) / jnp.maximum(center - lowest, 1e-06),
    )
    initial = factor / order * (center * identity - matrix) + occupied / order * identity

    def purify_step(index, density):
        square = jnp.dot(density, density, precision=PRECISE)
        cube = jnp.dot(square, density, precision=PRECISE)
        numerator = jnp.trace(square - cube)
        denominator = jnp.trace(density - square)
        safe_denominator = jnp.where(jnp.abs(denominator) > 1e-12, denominator, 1.0)
        ratio = jnp.clip(numerator / safe_denominator, 0.0, 1.0)
        upward = ((1.0 + ratio) * square - cube) / jnp.maximum(ratio, 0.5)
        downward = ((1.0 - 2.0 * ratio) * density + (1.0 + ratio) * square - cube) / jnp.maximum(
            1.0 - ratio, 0.5
        )
        return jnp.where(ratio >= 0.5, upward, downward)

    return lax.fori_loop(0, steps_count, purify_step, initial)


def ritz_basis(gram_stiff, gram_mass, modes_wanted, steps_count):
    order = gram_stiff.shape[0]
    gram_stiff = 0.5 * (gram_stiff + gram_stiff.T)
    gram_mass = 0.5 * (gram_mass + gram_mass.T)
    scaling = lax.rsqrt(jnp.diagonal(gram_mass) + 1e-06)
    stiff_scaled = scaling[:, None] * gram_stiff * scaling[None, :]
    mass_scaled = scaling[:, None] * gram_mass * scaling[None, :]
    factor_low = jnp.linalg.cholesky(mass_scaled)
    identity = jnp.eye(order, dtype=gram_stiff.dtype)
    inverse_low = lax.linalg.triangular_solve(factor_low, identity, left_side=True, lower=True)
    reduced = jnp.dot(
        jnp.dot(inverse_low, stiff_scaled, precision=PRECISE), inverse_low.T, precision=PRECISE
    )
    reduced = 0.5 * (reduced + reduced.T)
    if order > modes_wanted:
        projector = purify(reduced, modes_wanted, steps_count)
        columns = projector[:, :modes_wanted]
    else:
        columns = identity
    correlation = jnp.dot(columns.T, columns, precision=PRECISE)
    correlation_low = jnp.linalg.cholesky(correlation)
    orthonormal = lax.linalg.triangular_solve(
        correlation_low, columns.T, left_side=True, lower=True
    ).T
    coefficients = scaling[:, None] * jnp.dot(inverse_low.T, orthonormal, precision=PRECISE)
    projected = jnp.dot(
        jnp.dot(orthonormal.T, reduced, precision=PRECISE), orthonormal, precision=PRECISE
    )
    return (coefficients, 0.5 * (projected + projected.T))


def local(diag_blocks, coupling, offsets, mass, initial_modes):
    stiff_diag = jnp.diagonal(diag_blocks, axis1=1, axis2=2).reshape(-1)

    def gram_pair(basis, stiff_basis):
        local_stiff = jnp.dot(basis, stiff_basis.T, precision=PRECISE)
        local_mass = jnp.dot(basis * mass[None, :], basis.T, precision=PRECISE)
        return (one_axis_at_a_time(local_stiff, ROW), one_axis_at_a_time(local_mass, ROW))

    stiff_initial = stiffness_apply(initial_modes, diag_blocks, coupling, offsets)
    gram_stiff, gram_mass = gram_pair(initial_modes, stiff_initial)
    coefficients, projected = ritz_basis(gram_stiff, gram_mass, MODES, PURIFY)
    modes_now = jnp.dot(coefficients.T, initial_modes, precision=PRECISE)
    stiff_modes = jnp.dot(coefficients.T, stiff_initial, precision=PRECISE)
    directions = None
    stiff_directions = None
    for iteration in range(ITERS):
        residual = stiff_modes - jnp.dot(projected, modes_now * mass[None, :], precision=PRECISE)
        precond = residual / stiff_diag[None, :]
        stiff_precond = stiffness_apply(precond, diag_blocks, coupling, offsets)
        if directions is None:
            basis = jnp.concatenate([modes_now, precond], axis=0)
            stiff_basis = jnp.concatenate([stiff_modes, stiff_precond], axis=0)
        else:
            basis = jnp.concatenate([modes_now, precond, directions], axis=0)
            stiff_basis = jnp.concatenate([stiff_modes, stiff_precond, stiff_directions], axis=0)
        gram_stiff, gram_mass = gram_pair(basis, stiff_basis)
        coefficients, projected = ritz_basis(gram_stiff, gram_mass, MODES, PURIFY)
        directions = jnp.dot(coefficients[MODES:].T, basis[MODES:], precision=PRECISE)
        stiff_directions = jnp.dot(coefficients[MODES:].T, stiff_basis[MODES:], precision=PRECISE)
        modes_now = jnp.dot(coefficients.T, basis, precision=PRECISE)
        stiff_modes = jnp.dot(coefficients.T, stiff_basis, precision=PRECISE)
    weight = mass.shape[0] * lax.axis_size(ROW) / MODES
    mass_density = weight * mass * jnp.sum(modes_now * modes_now, axis=0)
    energy_density = weight * jnp.sum(modes_now * stiff_modes, axis=0)
    return (mass_density, energy_density)


def solution(mesh):
    torus = Mesh(
        mesh.devices.reshape(mesh.shape["sub"], 8, 8, 2), ("sub", "row_0", "row_1", "row_2")
    )
    return jax.shard_map(
        local,
        mesh=torus,
        in_specs=(
            P(SUB_ROW, None, None),
            P(SUB_ROW, None, None, None),
            P(SUB_ROW, None),
            P(SUB_ROW),
            P(None, SUB_ROW),
        ),
        out_specs=(P(SUB_ROW), P(SUB_ROW)),
        check_vma=False,
    )
```

profile of v0, /device:TPU:513, one launch (start us, length us, event | category | flops | bytes accessed | tf_op | source)
XLA Modules:
  0.0 1041.2 jit_solution(16284260710776054212)
XLA Ops:
  8.9 4.6 collective-permute-start
  19.0 19.7 %collective-permute-start.1 = (f32[32,512]{1,0:T(8,128)}, f32[32,512]{1,0:T(8,128)}, u32[]{:S(2)}, u32[]{:S(2)}) collective-permute-start(f32[32,512]{1,0:T(8,128)} %copy_bitcast_fusion.10), channel_id=1, source_target_pairs={{1,0},{2,1},{3,2},{4,3},{5,4},{6,5},{7,6},{8,7},{9,8},{10,9},{11,1... | collective-permute-start | bytes 196616 | tf_op jit(solution)/shard_map/ppermute | solution.py:19
  46.2 6.0 copy.58
  60.5 3.6 convolution_bitcast_fusion.8
  67.1 20.2 %all-reduce.7 = (f32[32,32]{1,0:T(8,128)S(1)}, f32[32,32]{1,0:T(8,128)S(1)}) all-reduce(f32[32,32]{1,0:T(8,128)S(1)} %fusion.60, f32[32,32]{1,0:T(8,128)S(1)} %convolution_bitcast_fusion.9), channel_id=1, replica_groups=mesh['sub'=2,'row_0'=8,'row_1'=8,'row_2'=2] {'row_0'}, use_global_device_ids=true, to_apply=%region_0.1 | all-reduce | flops 2048 | bytes 16384 | tf_op jit(solution)/shard_map/psum | solution.py:24
  87.3 20.3 %all-reduce.3 = (f32[32,32]{1,0:T(8,128)S(1)}, f32[32,32]{1,0:T(8,128)S(1)}) all-reduce(f32[32,32]{1,0:T(8,128)S(1)} %get-tuple-element.143, f32[32,32]{1,0:T(8,128)S(1)} %get-tuple-element.144), channel_id=1, replica_groups=mesh['sub'=2,'row_0'=8,'row_1'=8,'row_2'=2] {'row_1'}, use_global_device_ids=true, to_apply=%region_1.2 | all-reduce | flops 2048 | bytes 16384 | tf_op jit(solution)/shard_map/psum | solution.py:24
  107.6 16.7 %all-reduce.11 = (f32[32,32]{1,0:T(8,128)S(1)}, f32[32,32]{1,0:T(8,128)S(1)}) all-reduce(f32[32,32]{1,0:T(8,128)S(1)} %get-tuple-element.135, f32[32,32]{1,0:T(8,128)S(1)} %get-tuple-element.136), channel_id=1, replica_groups=mesh['sub'=2,'row_0'=8,'row_1'=8,'row_2'=2] {'row_2'}, use_global_device_ids=true, to_apply=%region_2.3 | all-reduce | flops 2048 | bytes 16384 | tf_op jit(solution)/shard_map/psum | solution.py:24
  138.0 2.9 fusion.74
  154.5 4.6 fusion.17
  161.2 20.8 %all-reduce.6 = (f32[64,64]{1,0:T(8,128)S(1)}, f32[64,64]{1,0:T(8,128)S(1)}) all-reduce(f32[64,64]{1,0:T(8,128)S(1)} %fusion.35, f32[64,64]{1,0:T(8,128)S(1)} %fusion.49), channel_id=1, replica_groups=mesh['sub'=2,'row_0'=8,'row_1'=8,'row_2'=2] {'row_0'}, use_global_device_ids=true, to_apply=%region_8.11 | all-reduce | flops 8192 | bytes 65536 | tf_op jit(solution)/shard_map/psum | solution.py:24
  182.0 23.7 %all-reduce.2 = (f32[64,64]{1,0:T(8,128)S(1)}, f32[64,64]{1,0:T(8,128)}) all-reduce(f32[64,64]{1,0:T(8,128)S(1)} %get-tuple-element.141, f32[64,64]{1,0:T(8,128)S(1)} %get-tuple-element.142), channel_id=1, replica_groups=mesh['sub'=2,'row_0'=8,'row_1'=8,'row_2'=2] {'row_1'}, use_global_device_ids=true, to_apply=%region_9.12 | all-reduce | flops 8192 | bytes 65536 | tf_op jit(solution)/shard_map/psum | solution.py:24
  205.6 19.7 %all-reduce.10 = (f32[64,64]{1,0:T(8,128)S(1)}, f32[64,64]{1,0:T(8,128)S(1)}) all-reduce(f32[64,64]{1,0:T(8,128)S(1)} %get-tuple-element.133, f32[64,64]{1,0:T(8,128)} %get-tuple-element.134), channel_id=1, replica_groups=mesh['sub'=2,'row_0'=8,'row_1'=8,'row_2'=2] {'row_2'}, use_global_device_ids=true, to_apply=%region_10.13 | all-reduce | flops 8192 | bytes 65536 | tf_op jit(solution)/shard_map/psum | solution.py:24
  228.3 5.8 cholesky.60
  235.6 4.9 custom-call.22
  245.7 81.9 %while.34 = (s32[]{:T(128)}, f32[64,64]{1,0:T(8,128)S(1)}, s32[]{:T(128)}, f32[]{:T(128)}, f32[]{:T(128)}, /*index=5*/f32[]{:T(128)}, f32[]{:T(128)}, f32[]{:T(128)}) while((s32[]{:T(128)}, f32[64,64]{1,0:T(8,128)S(1)}, s32[]{:T(128)}, f32[]{:T(128)}, f32[]{:T(128)}, /*index=5*/f32[]{:T(128)}, f32[]{:T(128)}, f32[]{:T(128)}) %tuple.100), condition=%wide.region_23.26_spmd, body=%wide.region_20.25_spmd.sunk | while | flops 6352909 | bytes 147713 | solution.py:80
  341.7 3.0 fusion.71
  359.4 4.6 fusion.14
  367.2 75.7 %all-reduce.25.cloned.1.call-done = (f32[96,96]{1,0:T(8,128)}, f32[96,96]{1,0:T(8,128)}) async-done(((f32[96,96]{1,0:T(8,128)}, f32[96,96]{1,0:T(8,128)}), (f32[96,96]{1,0:T(8,128)}, f32[96,96]{1,0:T(8,128)})) %all-reduce.25.cloned.1.call-update) | async-done | bytes 73744 | tf_op jit(solution)/shard_map/psum | solution.py:24
  443.1 75.6 %all-reduce.21.cloned.1.call-done = (f32[96,96]{1,0:T(8,128)}, f32[96,96]{1,0:T(8,128)}) async-done(((f32[96,96]{1,0:T(8,128)}, f32[96,96]{1,0:T(8,128)}), (f32[96,96]{1,0:T(8,128)}, f32[96,96]{1,0:T(8,128)})) %all-reduce.21.cloned.1.call-update) | async-done | bytes 73744 | tf_op jit(solution)/shard_map/psum | solution.py:24
  518.8 38.9 %all-reduce.29.cloned.1.call-done = (f32[96,96]{1,0:T(8,128)}, f32[96,96]{1,0:T(8,128)}) async-done(((f32[96,96]{1,0:T(8,128)}, f32[96,96]{1,0:T(8,128)}), (f32[96,96]{1,0:T(8,128)}, f32[96,96]{1,0:T(8,128)})) %all-reduce.29.cloned.1.call-update) | async-done | bytes 73744 | tf_op jit(solution)/shard_map/psum | solution.py:24
  561.8 8.8 cholesky.205
  571.9 7.4 custom-call.45
  586.0 89.0 %while.35 = (s32[]{:T(128)}, f32[96,96]{1,0:T(8,128)S(1)}, s32[]{:T(128)}, f32[]{:T(128)}, f32[]{:T(128)}, /*index=5*/f32[]{:T(128)}, f32[]{:T(128)}, f32[]{:T(128)}) while((s32[]{:T(128)}, f32[96,96]{1,0:T(8,128)S(1)}, s32[]{:T(128)}, f32[]{:T(128)}, f32[]{:T(128)}, /*index=5*/f32[]{:T(128)}, f32[]{:T(128)}, f32[]{:T(128)}) %tuple.103), condition=%wide.region_39.44_spmd, body=%wide.region_36.43_spmd.sunk | while | flops 21371904 | bytes 332033 | solution.py:80
  676.0 3.6 cholesky.216
  691.3 3.0 fusion.68
  709.9 4.6 fusion.11
  717.6 73.0 %all-reduce.23.cloned.1.call-done = (f32[96,96]{1,0:T(8,128)}, f32[96,96]{1,0:T(8,128)}) async-done(((f32[96,96]{1,0:T(8,128)}, f32[96,96]{1,0:T(8,128)}), (f32[96,96]{1,0:T(8,128)}, f32[96,96]{1,0:T(8,128)})) %all-reduce.23.cloned.1.call-update) | async-done | bytes 73744 | tf_op jit(solution)/shard_map/psum | solution.py:24
  791.1 75.2 %all-reduce.19.cloned.1.call-done = (f32[96,96]{1,0:T(8,128)}, f32[96,96]{1,0:T(8,128)}) async-done(((f32[96,96]{1,0:T(8,128)}, f32[96,96]{1,0:T(8,128)}), (f32[96,96]{1,0:T(8,128)}, f32[96,96]{1,0:T(8,128)})) %all-reduce.19.cloned.1.call-update) | async-done | bytes 73744 | tf_op jit(solution)/shard_map/psum | solution.py:24
  866.4 38.8 %all-reduce.27.cloned.1.call-done = (f32[96,96]{1,0:T(8,128)}, f32[96,96]{1,0:T(8,128)}) async-done(((f32[96,96]{1,0:T(8,128)}, f32[96,96]{1,0:T(8,128)}), (f32[96,96]{1,0:T(8,128)}, f32[96,96]{1,0:T(8,128)})) %all-reduce.27.cloned.1.call-update) | async-done | bytes 73744 | tf_op jit(solution)/shard_map/psum | solution.py:24
  909.8 9.6 cholesky.227
  920.7 8.0 custom-call.47
  937.8 83.4 %while.36 = (s32[]{:T(128)}, f32[96,96]{1,0:T(8,128)S(1)}, s32[]{:T(128)}, f32[]{:T(128)}, f32[]{:T(128)}, /*index=5*/f32[]{:T(128)}, f32[]{:T(128)}, f32[]{:T(128)}) while((s32[]{:T(128)}, f32[96,96]{1,0:T(8,128)S(1)}, s32[]{:T(128)}, f32[]{:T(128)}, f32[]{:T(128)}, /*index=5*/f32[]{:T(128)}, f32[]{:T(128)}, f32[]{:T(128)}) %tuple.106), condition=%wide.region_53.59_spmd, body=%wide.region_50.58_spmd.sunk | while | flops 21371904 | bytes 332033 | solution.py:80
  (565 shorter events, 247.0 us)
Async XLA Ops:
  7.2 8.0 copy-start
  7.2 435.7 %all-reduce.25.cloned.1.call-start = ((), (), s32[]{:S(2)}) async-start(), calls=%async_computation.3 | async-start | bytes 196608 | tf_op jit(solution)/shard_map/psum | solution.py:24
  8.9 46.7 %collective-permute-start = (f32[32,512]{1,0:T(8,128)}, f32[32,512]{1,0:T(8,128)}, u32[]{:S(2)}, u32[]{:S(2)}) collective-permute-start(f32[32,512]{1,0:T(8,128)} %slice.181), channel_id=1, source_target_pairs={{0,1},{1,2},{2,3},{3,4},{4,5},{5,6},{6,7},{7,8},{8,9},{9,10},{10,1... | collective-permute-start | bytes 196616 | tf_op jit(solution)/shard_map/ppermute | solution.py:19
  14.2 687.6 %copy-start.37 = (s32[16,3]{0,1:T(4,128)}, s32[16,3]{0,1:T(4,128)S(1)}, u32[]{:S(2)}) copy-start(s32[16,3]{0,1:T(4,128)S(1)} %subtract_add_fusion) | copy-start | bytes 580
  15.2 23.7 %copy-start.2 = (f32[32,2048]{1,0:T(8,128)S(1)}, f32[32,2048]{1,0:T(8,128)}, u32[]{:S(2)}) copy-start(f32[32,2048]{1,0:T(8,128)} %param.31) | copy-start | bytes 786436
  15.2 23.7 %copy-start.38 = (f32[2048]{0:T(1024)S(1)}, f32[2048]{0:T(1024)}, u32[]{:S(2)}) copy-start(f32[2048]{0:T(1024)} %param.30) | copy-start | bytes 24580
  18.3 20.4 %copy-start.22 = (f32[32,128,20]{1,0,2:T(8,128)}, f32[32,128,20]{1,0,2:T(8,128)S(1)}, u32[]{:S(2)}) copy-start(f32[32,128,20]{1,0,2:T(8,128)S(1)} %copy.223) | copy-start | bytes 983044
  19.0 46.2 %collective-permute-start.1 = (f32[32,512]{1,0:T(8,128)}, f32[32,512]{1,0:T(8,128)}, u32[]{:S(2)}, u32[]{:S(2)}) collective-permute-start(f32[32,512]{1,0:T(8,128)} %copy_bitcast_fusion.10), channel_id=1, source_target_pairs={{1,0},{2,1},{3,2},{4,3},{5,4},{6,5},{7,6},{8,7},{9,8},{10,9},{11,1... | collective-permute-start | bytes 196616 | tf_op jit(solution)/shard_map/ppermute | solution.py:19
  55.5 81.0 %copy-start.39 = (f32[16,128]{1,0:T(8,128)}, f32[16,128]{1,0:T(8,128)S(1)}, u32[]{:S(2)}) copy-start(f32[16,128]{1,0:T(8,128)S(1)} %copy.59) | copy-start | bytes 24580
  141.0 9.4 collective-permute-start.2
  148.3 10.8 %collective-permute-start.3 = (f32[32,512]{1,0:T(8,128)}, f32[32,512]{1,0:T(8,128)S(1)}, u32[]{:S(2)}, u32[]{:S(2)}) collective-permute-start(f32[32,512]{1,0:T(8,128)} %copy_bitcast_fusion.9), channel_id=1, source_target_pairs={{1,0},{2,1},{3,2},{4,3},{5,4},{6,5},{7,6},{8,7},{9,8},{10,9},{11,1... | collective-permute-start | bytes 196616 | tf_op jit(solution)/shard_map/ppermute | solution.py:19
  341.7 15.4 %copy-start.3 = (f32[32,2048]{1,0:T(8,128)}, f32[32,2048]{1,0:T(8,128)S(1)}, u32[]{:S(2)}) copy-start(f32[32,2048]{1,0:T(8,128)S(1)} %fusion.1) | copy-start | bytes 786436
  347.2 8.4 copy-start.12
  347.2 9.8 collective-permute-start.4
  353.5 10.5 %collective-permute-start.5 = (f32[32,512]{1,0:T(8,128)}, f32[32,512]{1,0:T(8,128)}, u32[]{:S(2)}, u32[]{:S(2)}) collective-permute-start(f32[32,512]{1,0:T(8,128)} %copy_bitcast_fusion.8), channel_id=1, source_target_pairs={{1,0},{2,1},{3,2},{4,3},{5,4},{6,5},{7,6},{8,7},{9,8},{10,9},{11,1... | collective-permute-start | bytes 196616 | tf_op jit(solution)/shard_map/ppermute | solution.py:19
  367.1 151.6 %all-reduce.21.cloned.1.call-start = ((), (), s32[]{:S(2)}) async-start(), calls=%async_computation.1 | async-start | bytes 196608 | tf_op jit(solution)/shard_map/psum | solution.py:24
  443.0 114.8 %all-reduce.29.cloned.1.call-start = ((), (), s32[]{:S(2)}) async-start(), calls=%async_computation.5 | async-start | bytes 196608 | tf_op jit(solution)/shard_map/psum | solution.py:24
  518.8 271.9 %all-reduce.23.cloned.1.call-start = ((), (), s32[]{:S(2)}) async-start(), calls=%async_computation.2 | async-start | bytes 196608 | tf_op jit(solution)/shard_map/psum | solution.py:24
  560.8 25.3 %copy-start.42 = (f32[96]{0:T(128)}, f32[96]{0:T(128)S(1)}, u32[]{:S(2)}) copy-start(f32[96]{0:T(128)S(1)} %get-tuple-element.165) | copy-start | bytes 1156
  675.0 21.4 %copy-start.5 = (f32[32,2048]{1,0:T(8,128)S(1)}, f32[32,2048]{1,0:T(8,128)}, u32[]{:S(2)}) copy-start(f32[32,2048]{1,0:T(8,128)} %copy-done.3) | copy-start | bytes 786436
  691.3 16.1 %copy-start.8 = (f32[32,2048]{1,0:T(8,128)}, f32[32,2048]{1,0:T(8,128)S(1)}, u32[]{:S(2)}) copy-start(f32[32,2048]{1,0:T(8,128)S(1)} %fusion) | copy-start | bytes 786436
  696.9 9.1 copy-start.28
  696.9 10.5 %collective-permute-start.6 = (f32[32,512]{1,0:T(8,128)S(1)}, f32[32,512]{1,0:T(8,128)S(1)}, u32[]{:S(2)}, u32[]{:S(2)}) collective-permute-start(f32[32,512]{1,0:T(8,128)S(1)} %slice.231), channel_id=1, source_target_pairs={{0,1},{1,2},{2,3},{3,4},{4,5},{5,6},{6,7},{7,8},{8,9},{9,10},{10,1... | collective-permute-start | bytes 196616 | tf_op jit(solution)/shard_map/ppermute | solution.py:19
  704.0 10.5 %collective-permute-start.7 = (f32[32,512]{1,0:T(8,128)}, f32[32,512]{1,0:T(8,128)}, u32[]{:S(2)}, u32[]{:S(2)}) collective-permute-start(f32[32,512]{1,0:T(8,128)} %copy_bitcast_fusion.7), channel_id=1, source_target_pairs={{1,0},{2,1},{3,2},{4,3},{5,4},{6,5},{7,6},{8,7},{9,8},{10,9},{11,1... | collective-permute-start | bytes 196616 | tf_op jit(solution)/shard_map/ppermute | solution.py:19
  708.2 7.9 copy-start.9
  708.2 7.9 copy-start.24
  708.2 7.9 copy-start.29
  708.2 7.9 copy-start.31
  708.2 7.9 copy-start.33
  717.6 148.7 %all-reduce.19.cloned.1.call-start = ((), (), s32[]{:S(2)}) async-start(), calls=%async_computation | async-start | bytes 196608 | tf_op jit(solution)/shard_map/psum | solution.py:24
  790.7 114.5 %all-reduce.27.cloned.1.call-start = ((), (), s32[]{:S(2)}) async-start(), calls=%async_computation.4 | async-start | bytes 196608 | tf_op jit(solution)/shard_map/psum | solution.py:24
  908.2 29.5 %copy-start.40 = (f32[96]{0:T(128)}, f32[96]{0:T(128)S(1)}, u32[]{:S(2)}) copy-start(f32[96]{0:T(128)S(1)} %get-tuple-element.163) | copy-start | bytes 1156
  (26 other events, 99.1 us)
Sparse Core Ops, SparseCore 0:
  367.2 75.6 all-reduce.24
  445.4 73.2 all-reduce.20
  521.3 36.3 all-reduce.28
  717.7 72.9 all-reduce.22
  793.0 73.2 all-reduce.18
  868.8 36.3 all-reduce.26
where the time goes:
time: 1050 us; the launch traced here: 1040 us
  waiting for transfers between devices  378 us (36%)
  matrix products  173 us (16%)
  loops' own time  168 us (16%)
  blocking collectives  121 us (12%)
  other arithmetic  101 us (10%)
  local copies, waits for them, and re-layouts  39.7 us (4%)
  starting transfers between devices  38.4 us (4%)
  between operations  22.1 us (2%)
    psum x6, waiting for transfers between devices, one_axis_at_a_time(): value = lax.psum(value, axis)  377 us
    another operation x3, loops' own time, purify(): return lax.fori_loop(0, steps_count, purify_step, initial)  168 us
    psum x6, blocking collectives, one_axis_at_a_time(): value = lax.psum(value, axis)  121 us
    dot_general x84, matrix products, purify_step(): cube = jnp.dot(square, density, precision=PRECISE)  69.6 us
    ppermute x8, starting transfers between devices, from_behind(): lax.ppermute(value, axis, [(source, source + steps) for source in range(i...  37.8 us
    another operation x12, other arithmetic, ritz_basis(): factor_low = jnp.linalg.cholesky(mass_scaled)  30 us
    another operation x8, other arithmetic, ritz_basis(): lax.linalg.triangular_solve(factor_low, identity, left_side=True, lower=T...  25.2 us
  transfers between devices with their start and end apart: 14, of which 6 were waited for; matrix products, arithmetic and copies ran while one was open for 7% of the time, Pallas kernels for 0%

commit v1 on v0

--- a/solution.py
+++ b/solution.py
@@ -21,7 +21,8 @@
 
 def one_axis_at_a_time(value, axes):
     for axis in axes:
-        value = lax.psum(value, axis)
+        pieces = lax.all_gather(value, axis, axis=0, tiled=False)
+        value = pieces.sum(axis=0)
     return value
 
 

time: 1050 us -> 998 us (0.950)
  waiting for transfers between devices: 378 us -> 0.03 us
  blocking collectives: 121 us -> 450 us
  other arithmetic: 101 us -> 123 us
  between operations: 22.1 us -> 8.3 us
    all_gather x0 -> x24, blocking collectives: none -> 450 us  [one_axis_at_a_time(): pieces = lax.all_gather(value, axis, axis=0, tiled=False)]
    psum x6 -> x0, waiting for transfers between devices: 377 us -> none  [one_axis_at_a_time(): value = lax.psum(value, axis)]
    psum x6 -> x0, blocking collectives: 121 us -> none  [one_axis_at_a_time(): value = lax.psum(value, axis)]
    reduce_sum x0 -> x24, other arithmetic: none -> 16.1 us  [one_axis_at_a_time(): value = pieces.sum(axis=0)]
  transfers between devices with their start and end apart: 14 -> 8, of which waited for: 6 -> 0; matrix products, arithmetic and copies ran while one was open for 7% -> 15% of each run, Pallas kernels for 0% -> 0%
where the time goes in v1:
time: 998 us; the launch traced here: 988 us
  blocking collectives  450 us (45%)
  matrix products  171 us (17%)
  loops' own time  159 us (16%)
  other arithmetic  123 us (12%)
  starting transfers between devices  39.3 us (4%)
  local copies, waits for them, and re-layouts  37.8 us (4%)
    all_gather x24, blocking collectives, one_axis_at_a_time(): pieces = lax.all_gather(value, axis, axis=0, tiled=False)  450 us
    another operation x3, loops' own time, purify(): return lax.fori_loop(0, steps_count, purify_step, initial)  159 us
    dot_general x84, matrix products, purify_step(): cube = jnp.dot(square, density, precision=PRECISE)  67.9 us
    ppermute x8, starting transfers between devices, from_behind(): lax.ppermute(value, axis, [(source, source + steps) for source in range(i...  39.3 us
    another operation x12, other arithmetic, ritz_basis(): factor_low = jnp.linalg.cholesky(mass_scaled)  30.6 us
    another operation x8, other arithmetic, ritz_basis(): lax.linalg.triangular_solve(factor_low, identity, left_side=True, lower=T...  25.2 us
  transfers between devices with their start and end apart: 8, of which 0 were waited for; matrix products, arithmetic and copies ran while one was open for 15% of the time, Pallas kernels for 0%

profile of v1, /device:TPU:513, one launch (start us, length us, event | category | flops | bytes accessed | tf_op | source)
XLA Modules:
  0.0 987.8 jit_solution(11650982703895137587)
XLA Ops:
  12.4 19.7 %collective-permute-start.1 = (f32[32,512]{1,0:T(8,128)}, f32[32,512]{1,0:T(8,128)}, u32[]{:S(2)}, u32[]{:S(2)}) collective-permute-start(f32[32,512]{1,0:T(8,128)} %copy_bitcast_fusion.10), channel_id=1, source_target_pairs={{1,0},{2,1},{3,2},{4,3},{5,4},{6,5},{7,6},{8,7},{9,8},{10,9},{11,1... | collective-permute-start | bytes 196616 | tf_op jit(solution)/shard_map/ppermute | solution.py:19
  32.6 20.6 %all-gather = f32[256,32]{1,0:T(8,128)} all-gather(f32[32,32]{1,0:T(8,128)S(1)} %fusion.48), channel_id=2, replica_groups=mesh['sub'=2,'row_0'=8,'row_1'=8,'row_2'=2] {'row_0'}, dimensions={0}, use_global_device_ids=true | all-gather | bytes 36864 | tf_op jit(solution)/shard_map/all_gather | solution.py:24
  54.1 20.3 %all-gather.1 = f32[256,32]{1,0:T(8,128)} all-gather(f32[32,32]{1,0:T(8,128)S(1)} %reduce_sum.332), channel_id=3, replica_groups=mesh['sub'=2,'row_0'=8,'row_1'=8,'row_2'=2] {'row_1'}, dimensions={0}, use_global_device_ids=true | all-gather | bytes 36864 | tf_op jit(solution)/shard_map/all_gather | solution.py:24
  75.3 13.8 %all-gather.2 = f32[64,32]{1,0:T(8,128)S(1)} all-gather(f32[32,32]{1,0:T(8,128)S(1)} %reduce_sum.333), channel_id=4, replica_groups=mesh['sub'=2,'row_0'=8,'row_1'=8,'row_2'=2] {'row_2'}, dimensions={0}, use_global_device_ids=true | all-gather | bytes 12288 | tf_op jit(solution)/shard_map/all_gather | solution.py:24
  125.9 18.3 %all-gather.3 = f32[256,32]{1,0:T(8,128)S(1)} all-gather(f32[32,32]{1,0:T(8,128)S(1)} %copy.286), channel_id=5, replica_groups=mesh['sub'=2,'row_0'=8,'row_1'=8,'row_2'=2] {'row_0'}, dimensions={0}, use_global_device_ids=true | all-gather | bytes 36864 | tf_op jit(solution)/shard_map/all_gather | solution.py:24
  144.2 18.3 %all-gather.4 = f32[256,32]{1,0:T(8,128)S(1)} all-gather(f32[32,32]{1,0:T(8,128)S(1)} %reduce_sum.335), channel_id=6, replica_groups=mesh['sub'=2,'row_0'=8,'row_1'=8,'row_2'=2] {'row_1'}, dimensions={0}, use_global_device_ids=true | all-gather | bytes 36864 | tf_op jit(solution)/shard_map/all_gather | solution.py:24
  162.5 14.7 %all-gather.5 = f32[64,32]{1,0:T(8,128)S(1)} all-gather(f32[32,32]{1,0:T(8,128)S(1)} %reduce_sum.336), channel_id=7, replica_groups=mesh['sub'=2,'row_0'=8,'row_1'=8,'row_2'=2] {'row_2'}, dimensions={0}, use_global_device_ids=true | all-gather | bytes 12288 | tf_op jit(solution)/shard_map/all_gather | solution.py:24
  194.3 20.6 %all-gather.6 = f32[512,64]{1,0:T(8,128)} all-gather(f32[64,64]{1,0:T(8,128)S(1)} %fusion.27), channel_id=8, replica_groups=mesh['sub'=2,'row_0'=8,'row_1'=8,'row_2'=2] {'row_0'}, dimensions={0}, use_global_device_ids=true | all-gather | bytes 147456 | tf_op jit(solution)/shard_map/all_gather | solution.py:24
  215.8 20.9 %all-gather.7 = f32[512,64]{1,0:T(8,128)} all-gather(f32[64,64]{1,0:T(8,128)S(1)} %reduce_sum.338), channel_id=9, replica_groups=mesh['sub'=2,'row_0'=8,'row_1'=8,'row_2'=2] {'row_1'}, dimensions={0}, use_global_device_ids=true | all-gather | bytes 147456 | tf_op jit(solution)/shard_map/all_gather | solution.py:24
  237.7 15.8 %all-gather.8 = f32[128,64]{1,0:T(8,128)S(1)} all-gather(f32[64,64]{1,0:T(8,128)S(1)} %reduce_sum.339), channel_id=10, replica_groups=mesh['sub'=2,'row_0'=8,'row_1'=8,'row_2'=2] {'row_2'}, dimensions={0}, use_global_device_ids=true | all-gather | bytes 49152 | tf_op jit(solution)/shard_map/all_gather | solution.py:24
  278.5 20.4 %all-gather.9 = f32[512,64]{1,0:T(8,128)} all-gather(f32[64,64]{1,0:T(8,128)S(1)} %fusion.41), channel_id=11, replica_groups=mesh['sub'=2,'row_0'=8,'row_1'=8,'row_2'=2] {'row_0'}, dimensions={0}, use_global_device_ids=true | all-gather | bytes 147456 | tf_op jit(solution)/shard_map/all_gather | solution.py:24
  299.9 20.5 %all-gather.10 = f32[512,64]{1,0:T(8,128)} all-gather(f32[64,64]{1,0:T(8,128)S(1)} %reduce_sum.341), channel_id=12, replica_groups=mesh['sub'=2,'row_0'=8,'row_1'=8,'row_2'=2] {'row_1'}, dimensions={0}, use_global_device_ids=true | all-gather | bytes 147456 | tf_op jit(solution)/shard_map/all_gather | solution.py:24
  321.4 15.0 %all-gather.11 = f32[128,64]{1,0:T(8,128)S(1)} all-gather(f32[64,64]{1,0:T(8,128)S(1)} %reduce_sum.342), channel_id=13, replica_groups=mesh['sub'=2,'row_0'=8,'row_1'=8,'row_2'=2] {'row_2'}, dimensions={0}, use_global_device_ids=true | all-gather | bytes 49152 | tf_op jit(solution)/shard_map/all_gather | solution.py:24
  341.2 81.4 %while.34 = (s32[]{:T(128)}, f32[64,64]{1,0:T(8,128)S(1)}, s32[]{:T(128)}, f32[]{:T(128)}, f32[]{:T(128)}, /*index=5*/f32[]{:T(128)}, f32[]{:T(128)}, f32[]{:T(128)}) while((s32[]{:T(128)}, f32[64,64]{1,0:T(8,128)S(1)}, s32[]{:T(128)}, f32[]{:T(128)}, f32[]{:T(128)}, /*index=5*/f32[]{:T(128)}, f32[]{:T(128)}, f32[]{:T(128)}) %tuple.108), condition=%wide.region_23.26_spmd, body=%wide.region_20.25_spmd.sunk | while | flops 6352909 | bytes 147713 | solution.py:81
  452.7 20.8 %all-gather.12 = f32[768,96]{1,0:T(8,128)} all-gather(f32[96,96]{1,0:T(8,128)S(1)} %fusion.5), channel_id=14, replica_groups=mesh['sub'=2,'row_0'=8,'row_1'=8,'row_2'=2] {'row_0'}, dimensions={0}, use_global_device_ids=true | all-gather | bytes 331776 | tf_op jit(solution)/shard_map/all_gather | solution.py:24
  474.5 21.2 %all-gather.13 = f32[768,96]{1,0:T(8,128)} all-gather(f32[96,96]{1,0:T(8,128)S(1)} %reduce_sum.346), channel_id=15, replica_groups=mesh['sub'=2,'row_0'=8,'row_1'=8,'row_2'=2] {'row_1'}, dimensions={0}, use_global_device_ids=true | all-gather | bytes 331776 | tf_op jit(solution)/shard_map/all_gather | solution.py:24
  496.7 18.1 %all-gather.14 = f32[192,96]{1,0:T(8,128)} all-gather(f32[96,96]{1,0:T(8,128)S(1)} %reduce_sum.347), channel_id=16, replica_groups=mesh['sub'=2,'row_0'=8,'row_1'=8,'row_2'=2] {'row_2'}, dimensions={0}, use_global_device_ids=true | all-gather | bytes 110592 | tf_op jit(solution)/shard_map/all_gather | solution.py:24
  520.2 9.6 cholesky.205
  531.1 7.4 custom-call.45
  550.7 19.1 %all-gather.15 = f32[768,96]{1,0:T(8,128)S(1)} all-gather(f32[96,96]{1,0:T(8,128)S(1)} %fusion.31), channel_id=17, replica_groups=mesh['sub'=2,'row_0'=8,'row_1'=8,'row_2'=2] {'row_0'}, dimensions={0}, use_global_device_ids=true | all-gather | bytes 331776 | tf_op jit(solution)/shard_map/all_gather | solution.py:24
  570.5 19.3 %all-gather.16 = f32[768,96]{1,0:T(8,128)S(1)} all-gather(f32[96,96]{1,0:T(8,128)} %reduce_sum.349), channel_id=18, replica_groups=mesh['sub'=2,'row_0'=8,'row_1'=8,'row_2'=2] {'row_1'}, dimensions={0}, use_global_device_ids=true | all-gather | bytes 331776 | tf_op jit(solution)/shard_map/all_gather | solution.py:24
  590.5 14.2 %all-gather.17 = f32[192,96]{1,0:T(8,128)S(1)} all-gather(f32[96,96]{1,0:T(8,128)} %reduce_sum.350), channel_id=19, replica_groups=mesh['sub'=2,'row_0'=8,'row_1'=8,'row_2'=2] {'row_2'}, dimensions={0}, use_global_device_ids=true | all-gather | bytes 110592 | tf_op jit(solution)/shard_map/all_gather | solution.py:24
  611.1 78.1 %while.35 = (s32[]{:T(128)}, f32[96,96]{1,0:T(8,128)S(1)}, s32[]{:T(128)}, f32[]{:T(128)}, f32[]{:T(128)}, /*index=5*/f32[]{:T(128)}, f32[]{:T(128)}, f32[]{:T(128)}) while((s32[]{:T(128)}, f32[96,96]{1,0:T(8,128)S(1)}, s32[]{:T(128)}, f32[]{:T(128)}, f32[]{:T(128)}, /*index=5*/f32[]{:T(128)}, f32[]{:T(128)}, f32[]{:T(128)}) %tuple.111), condition=%wide.region_39.44_spmd, body=%wide.region_36.43_spmd.sunk | while | flops 21371904 | bytes 332033 | solution.py:81
  724.6 21.2 %all-gather.18 = f32[768,96]{1,0:T(8,128)} all-gather(f32[96,96]{1,0:T(8,128)S(1)} %fusion.3), channel_id=20, replica_groups=mesh['sub'=2,'row_0'=8,'row_1'=8,'row_2'=2] {'row_0'}, dimensions={0}, use_global_device_ids=true | all-gather | bytes 331776 | tf_op jit(solution)/shard_map/all_gather | solution.py:24
  746.8 21.1 %all-gather.19 = f32[768,96]{1,0:T(8,128)} all-gather(f32[96,96]{1,0:T(8,128)S(1)} %reduce_sum.354), channel_id=21, replica_groups=mesh['sub'=2,'row_0'=8,'row_1'=8,'row_2'=2] {'row_1'}, dimensions={0}, use_global_device_ids=true | all-gather | bytes 331776 | tf_op jit(solution)/shard_map/all_gather | solution.py:24
  768.9 18.4 %all-gather.20 = f32[192,96]{1,0:T(8,128)} all-gather(f32[96,96]{1,0:T(8,128)S(1)} %reduce_sum.355), channel_id=22, replica_groups=mesh['sub'=2,'row_0'=8,'row_1'=8,'row_2'=2] {'row_2'}, dimensions={0}, use_global_device_ids=true | all-gather | bytes 110592 | tf_op jit(solution)/shard_map/all_gather | solution.py:24
  792.7 9.6 cholesky.227
  803.6 8.0 custom-call.47
  824.0 21.3 %all-gather.21 = f32[768,96]{1,0:T(8,128)} all-gather(f32[96,96]{1,0:T(8,128)S(1)} %fusion.29), channel_id=23, replica_groups=mesh['sub'=2,'row_0'=8,'row_1'=8,'row_2'=2] {'row_0'}, dimensions={0}, use_global_device_ids=true | all-gather | bytes 331776 | tf_op jit(solution)/shard_map/all_gather | solution.py:24
  846.4 20.9 %all-gather.22 = f32[768,96]{1,0:T(8,128)} all-gather(f32[96,96]{1,0:T(8,128)S(1)} %reduce_sum.357), channel_id=24, replica_groups=mesh['sub'=2,'row_0'=8,'row_1'=8,'row_2'=2] {'row_1'}, dimensions={0}, use_global_device_ids=true | all-gather | bytes 331776 | tf_op jit(solution)/shard_map/all_gather | solution.py:24
  868.3 14.6 %all-gather.23 = f32[192,96]{1,0:T(8,128)} all-gather(f32[96,96]{1,0:T(8,128)S(1)} %reduce_sum.358), channel_id=25, replica_groups=mesh['sub'=2,'row_0'=8,'row_1'=8,'row_2'=2] {'row_2'}, dimensions={0}, use_global_device_ids=true | all-gather | bytes 110592 | tf_op jit(solution)/shard_map/all_gather | solution.py:24
  891.6 83.4 %while.36 = (s32[]{:T(128)}, f32[96,96]{1,0:T(8,128)S(1)}, s32[]{:T(128)}, f32[]{:T(128)}, f32[]{:T(128)}, /*index=5*/f32[]{:T(128)}, f32[]{:T(128)}, f32[]{:T(128)}) while((s32[]{:T(128)}, f32[96,96]{1,0:T(8,128)S(1)}, s32[]{:T(128)}, f32[]{:T(128)}, f32[]{:T(128)}, /*index=5*/f32[]{:T(128)}, f32[]{:T(128)}, f32[]{:T(128)}) %tuple.114), condition=%wide.region_53.59_spmd, body=%wide.region_50.58_spmd.sunk | while | flops 21371904 | bytes 332033 | solution.py:81
  (586 shorter events, 317.1 us)
Async XLA Ops:
  0.6 7.9 copy-start
  2.3 111.6 %collective-permute-start = (f32[32,512]{1,0:T(8,128)}, f32[32,512]{1,0:T(8,128)}, u32[]{:S(2)}, u32[]{:S(2)}) collective-permute-start(f32[32,512]{1,0:T(8,128)} %slice.181), channel_id=1, source_target_pairs={{0,1},{1,2},{2,3},{3,4},{4,5},{5,6},{6,7},{7,8},{8,9},{9,10},{10,1... | collective-permute-start | bytes 196616 | tf_op jit(solution)/shard_map/ppermute | solution.py:19
  7.5 710.7 %copy-start.34 = (s32[16,3]{0,1:T(4,128)}, s32[16,3]{0,1:T(4,128)S(1)}, u32[]{:S(2)}) copy-start(s32[16,3]{0,1:T(4,128)S(1)} %subtract_add_fusion) | copy-start | bytes 580
  8.5 23.7 %copy-start.2 = (f32[32,2048]{1,0:T(8,128)S(1)}, f32[32,2048]{1,0:T(8,128)}, u32[]{:S(2)}) copy-start(f32[32,2048]{1,0:T(8,128)} %param.31) | copy-start | bytes 786436
  8.6 23.7 %copy-start.36 = (f32[2048]{0:T(1024)S(1)}, f32[2048]{0:T(1024)}, u32[]{:S(2)}) copy-start(f32[2048]{0:T(1024)} %param.30) | copy-start | bytes 24580
  11.7 20.6 %copy-start.20 = (f32[32,128,20]{1,0,2:T(8,128)}, f32[32,128,20]{1,0,2:T(8,128)S(1)}, u32[]{:S(2)}) copy-start(f32[32,128,20]{1,0,2:T(8,128)S(1)} %copy.453) | copy-start | bytes 983044
  12.4 111.1 %collective-permute-start.1 = (f32[32,512]{1,0:T(8,128)}, f32[32,512]{1,0:T(8,128)}, u32[]{:S(2)}, u32[]{:S(2)}) collective-permute-start(f32[32,512]{1,0:T(8,128)} %copy_bitcast_fusion.10), channel_id=1, source_target_pairs={{1,0},{2,1},{3,2},{4,3},{5,4},{6,5},{7,6},{8,7},{9,8},{10,9},{11,1... | collective-permute-start | bytes 196616 | tf_op jit(solution)/shard_map/ppermute | solution.py:19
  122.4 55.7 %copy-start.39 = (f32[16,128]{1,0:T(8,128)S(1)}, f32[16,128]{1,0:T(8,128)}, u32[]{:S(2)}) copy-start(f32[16,128]{1,0:T(8,128)} %copy.296) | copy-start | bytes 24580
  184.8 82.5 %collective-permute-start.2 = (f32[32,512]{1,0:T(8,128)}, f32[32,512]{1,0:T(8,128)}, u32[]{:S(2)}, u32[]{:S(2)}) collective-permute-start(f32[32,512]{1,0:T(8,128)} %slice.221), channel_id=1, source_target_pairs={{0,1},{1,2},{2,3},{3,4},{4,5},{5,6},{6,7},{7,8},{8,9},{9,10},{10,1... | collective-permute-start | bytes 196616 | tf_op jit(solution)/shard_map/ppermute | solution.py:19
  191.2 85.7 %collective-permute-start.3 = (f32[32,512]{1,0:T(8,128)}, f32[32,512]{1,0:T(8,128)}, u32[]{:S(2)}, u32[]{:S(2)}) collective-permute-start(f32[32,512]{1,0:T(8,128)} %copy_bitcast_fusion.9), channel_id=1, source_target_pairs={{1,0},{2,1},{3,2},{4,3},{5,4},{6,5},{7,6},{8,7},{9,8},{10,9},{11,1... | collective-permute-start | bytes 196616 | tf_op jit(solution)/shard_map/ppermute | solution.py:19
  267.3 70.1 %copy-start.33 = (f32[64,64]{1,0:T(8,128)}, f32[64,64]{1,0:T(8,128)S(1)}, u32[]{:S(2)}) copy-start(f32[64,64]{1,0:T(8,128)S(1)} %fusion.121) | copy-start | bytes 49156
  277.8 21.1 %copy-start.16 = (f32[32,2048]{1,0:T(8,128)}, f32[32,2048]{1,0:T(8,128)S(1)}, u32[]{:S(2)}) copy-start(f32[32,2048]{1,0:T(8,128)S(1)} %copy_bitcast_fusion.6) | copy-start | bytes 786436
  436.9 14.9 %copy-start.3 = (f32[32,2048]{1,0:T(8,128)}, f32[32,2048]{1,0:T(8,128)S(1)}, u32[]{:S(2)}) copy-start(f32[32,2048]{1,0:T(8,128)S(1)} %fusion.1) | copy-start | bytes 786436
  443.0 8.8 copy-start.11
  443.0 96.4 %collective-permute-start.4 = (f32[32,512]{1,0:T(8,128)}, f32[32,512]{1,0:T(8,128)}, u32[]{:S(2)}, u32[]{:S(2)}) collective-permute-start(f32[32,512]{1,0:T(8,128)} %slice.226), channel_id=1, source_target_pairs={{0,1},{1,2},{2,3},{3,4},{4,5},{5,6},{6,7},{7,8},{8,9},{9,10},{10,1... | collective-permute-start | bytes 196616 | tf_op jit(solution)/shard_map/ppermute | solution.py:19
  448.7 100.3 %collective-permute-start.5 = (f32[32,512]{1,0:T(8,128)}, f32[32,512]{1,0:T(8,128)}, u32[]{:S(2)}, u32[]{:S(2)}) collective-permute-start(f32[32,512]{1,0:T(8,128)} %copy_bitcast_fusion.8), channel_id=1, source_target_pairs={{1,0},{2,1},{3,2},{4,3},{5,4},{6,5},{7,6},{8,7},{9,8},{10,9},{11,1... | collective-permute-start | bytes 196616 | tf_op jit(solution)/shard_map/ppermute | solution.py:19
  452.6 86.8 %copy-start.4 = (f32[32,2048]{1,0:T(8,128)S(1)}, f32[32,2048]{1,0:T(8,128)}, u32[]{:S(2)}) copy-start(f32[32,2048]{1,0:T(8,128)} %copy-done.3) | copy-start | bytes 786436
  542.8 7.2 copy-start.27
  607.0 99.4 %copy-start.38 = (f32[2048]{0:T(1024)S(1)}, f32[2048]{0:T(1024)}, u32[]{:S(2)}) copy-start(f32[2048]{0:T(1024)} %param.30) | copy-start | bytes 24580
  607.0 99.4 %copy-start.40 = (f32[16,128]{1,0:T(8,128)S(1)}, f32[16,128]{1,0:T(8,128)}, u32[]{:S(2)}) copy-start(f32[16,128]{1,0:T(8,128)} %copy.296) | copy-start | bytes 24580
  689.2 24.5 %copy-start.5 = (f32[32,2048]{1,0:T(8,128)S(1)}, f32[32,2048]{1,0:T(8,128)}, u32[]{:S(2)}) copy-start(f32[32,2048]{1,0:T(8,128)} %copy-done.3) | copy-start | bytes 786436
  706.4 7.3 copy-start.13
  707.9 15.8 %copy-start.7 = (f32[32,2048]{1,0:T(8,128)}, f32[32,2048]{1,0:T(8,128)S(1)}, u32[]{:S(2)}) copy-start(f32[32,2048]{1,0:T(8,128)S(1)} %fusion) | copy-start | bytes 786436
  714.1 9.6 copy-start.23
  714.1 98.5 %collective-permute-start.6 = (f32[32,512]{1,0:T(8,128)}, f32[32,512]{1,0:T(8,128)}, u32[]{:S(2)}, u32[]{:S(2)}) collective-permute-start(f32[32,512]{1,0:T(8,128)} %slice.231), channel_id=1, source_target_pairs={{0,1},{1,2},{2,3},{3,4},{4,5},{5,6},{6,7},{7,8},{8,9},{9,10},{10,1... | collective-permute-start | bytes 196616 | tf_op jit(solution)/shard_map/ppermute | solution.py:19
  716.1 7.6 copy-start.30
  720.5 95.5 %copy-start.35 = (s32[16,3]{0,1:T(4,128)S(1)}, s32[16,3]{0,1:T(4,128)}, u32[]{:S(2)}) copy-start(s32[16,3]{0,1:T(4,128)} %copy-done.34) | copy-start | bytes 580
  720.5 101.7 %collective-permute-start.7 = (f32[32,512]{1,0:T(8,128)}, f32[32,512]{1,0:T(8,128)}, u32[]{:S(2)}, u32[]{:S(2)}) collective-permute-start(f32[32,512]{1,0:T(8,128)} %copy_bitcast_fusion.7), channel_id=1, source_target_pairs={{1,0},{2,1},{3,2},{4,3},{5,4},{6,5},{7,6},{8,7},{9,8},{10,9},{11,1... | collective-permute-start | bytes 196616 | tf_op jit(solution)/shard_map/ppermute | solution.py:19
  724.5 88.1 %copy-start.8 = (f32[32,2048]{1,0:T(8,128)S(1)}, f32[32,2048]{1,0:T(8,128)}, u32[]{:S(2)}) copy-start(f32[32,2048]{1,0:T(8,128)} %copy-done.7) | copy-start | bytes 786436
  791.1 93.5 %copy-start.41 = (f32[96]{0:T(128)}, f32[96]{0:T(128)S(1)}, u32[]{:S(2)}) copy-start(f32[96]{0:T(128)S(1)} %get-tuple-element.155) | copy-start | bytes 1156
  812.6 73.0 %copy-start.32 = (f32[96,96]{1,0:T(8,128)}, f32[96,96]{1,0:T(8,128)S(1)}, u32[]{:S(2)}) copy-start(f32[96,96]{1,0:T(8,128)S(1)} %fusion.81) | copy-start | bytes 110596
  816.0 7.2 copy-start.31
  (19 other events, 90.0 us)
